TPU v7x, 32 devices: a whole 2x2x4 slice. The times are simulated.
32 devices in a mesh: section: 1, srv: 16 (over z, x, core), tp: 2 (over y).
Axes of the slice: x: 2, y: 2, z: 4, core: 2. Of those that a mesh axis runs over, the one named last changes fastest.
Arguments:
- queries: bfloat16 [2048, 4096], P(('section', 'srv'), 'tp'), may hold values from -40 to 40
- keys: bfloat16 [2048, 512], P(('section', 'srv'), 'tp'), may hold values from -40 to 40
- values: bfloat16 [2048, 512], P(('section', 'srv'), 'tp'), may hold values from -6 to 6
- residual: bfloat16 [2048, 4096], P(('section', 'srv'), 'tp'), may hold values from -6 to 6
- out_weight: bfloat16 [4096, 4096], P('tp', ('section', 'srv')), may hold values from -0.1875 to 0.1875
- norm_gain: float32 [4096], P('tp'), may hold values from 0.25 to 1.75
- level_shift: float32 [8, 4096], P(None, 'tp'), may hold values from -3 to 3
- doc_lengths: int32 [1, 4], P('section'), may hold values from 1 to 64, 128 in all within a row
- noise_level: int32 [1, 4], P('section'), may hold values from 0 to 7
Outputs:
- normed: bfloat16 [2048, 4096], P(('section', 'srv'), 'tp')
Inputs may be any that keep to these rules, and one draw needn't show every extreme that they name: `doc_lengths`: each micro-batch's lengths sum to 128.
All inputs are finite; a program needn't handle non-finite values.
Results may differ from a plain program's by a relative error of at most 0.013.
Values may be sent and summed in bfloat16 or wider, within the bound.
No kernel may reach another device: no remote copies, remote signals or barrier semaphores. Data moves between devices by JAX's collectives and lax.ppermute only.
A program may use at most 64 MiB of HBM per device.

v0:
```python
import jax
import jax.numpy as jnp
from jax import lax
from jax.sharding import PartitionSpec as P

D = 4096
HEAD_SIZE = 128
BLK = 16


def shifted(block, axis, distance):
    devices = range(lax.axis_size(axis))
    route = [(i - distance, i) for i in devices if i - distance in devices]
    return lax.ppermute(block, axis, route)


def bounds(positions, starts, ends):
    member = (positions[:, None] >= starts[None, :]) & (positions[:, None] < ends[None, :])
    first = jnp.sum(jnp.where(member, starts[None, :], 0), axis=1)
    limit = (positions // BLK + 1) * BLK
    return (member, first, limit)


def make_absorb(query_block, first, limit, kv_heads, query_groups):
    rows = query_block.shape[0]
    scale = HEAD_SIZE ** (-0.5)
    grouped = (
        query_block.reshape(rows, kv_heads, query_groups, HEAD_SIZE)
        .transpose(1, 2, 0, 3)
        .reshape(kv_heads, query_groups * rows, HEAD_SIZE)
    )
    row_first = jnp.tile(first, query_groups)
    row_limit = jnp.tile(limit, query_groups)
    empty = (
        jnp.full((kv_heads, query_groups * rows), -1e30, jnp.float32),
        jnp.zeros((kv_heads, query_groups * rows), jnp.float32),
        jnp.zeros((kv_heads, query_groups * rows, HEAD_SIZE), jnp.float32),
    )

    def absorb(carry, pieces, start):
        key_piece, value_piece = pieces
        count = key_piece.shape[0]
        key_pos = start + jnp.arange(count, dtype=jnp.int32)
        mask = (key_pos[None, :] >= row_first[:, None]) & (key_pos[None, :] < row_limit[:, None])

        def update(state):
            best, total, summed = state
            key_heads = key_piece.reshape(count, kv_heads, HEAD_SIZE)
            value_heads = value_piece.reshape(count, kv_heads, HEAD_SIZE)
            scores = (
                jnp.einsum("kxd,jkd->kxj", grouped, key_heads, preferred_element_type=jnp.float32)
                * scale
            )
            scores = jnp.where(mask[None], scores, -1e30)
            new_best = jnp.maximum(best, jnp.max(scores, axis=-1))
            weights = jnp.where(mask[None], jnp.exp(scores - new_best[..., None]), 0.0)
            factor = jnp.exp(best - new_best)
            total = total * factor + jnp.sum(weights, axis=-1)
            update_sum = jnp.einsum(
                "kxj,jkd->kxd",
                weights.astype(jnp.bfloat16),
                value_heads,
                preferred_element_type=jnp.float32,
            )
            return (new_best, total, summed * factor[..., None] + update_sum)

        return lax.cond(jnp.any(mask), update, lambda state: state, carry)

    return (absorb, empty)


def finish(carry, rows, kv_heads, query_groups):
    best, total, summed = carry
    attended = (
        (summed / total[..., None])
        .reshape(kv_heads, query_groups, rows, HEAD_SIZE)
        .transpose(2, 0, 1, 3)
    )
    return attended.reshape(rows, kv_heads * query_groups * HEAD_SIZE).astype(jnp.bfloat16)


def on_device(
    queries, keys, values, residual, out_weight, norm_gain, level_shift, doc_lengths, noise_level
):
    rows = queries.shape[0]
    kv_heads = keys.shape[1] // HEAD_SIZE
    query_groups = queries.shape[1] // keys.shape[1]
    here = lax.axis_index("srv")
    devices = lax.axis_size("srv")
    lengths = doc_lengths[0] * BLK
    ends = jnp.cumsum(lengths)
    starts = ends - lengths
    positions = here * rows + jnp.arange(rows, dtype=jnp.int32)
    member, first, limit = bounds(positions, starts, ends)
    absorb, empty = make_absorb(queries, first, limit, kv_heads, query_groups)
    span = min(devices, devices // 2 + 1)
    carry = absorb(empty, (keys, values), here * rows)

    def turn_step(turn, state):
        carry_now, held = state
        held = shifted(held, "srv", 1)
        carry_now = absorb(carry_now, (held[0], held[1]), (here - turn) * rows)
        return (carry_now, held)

    carry, held = lax.fori_loop(1, span, turn_step, (carry, jnp.stack([keys, values], axis=0)))
    attended = finish(carry, rows, kv_heads, query_groups)
    partial_sum = jnp.dot(
        attended,
        lax.all_gather(out_weight, ("section", "srv"), axis=1, tiled=True),
        preferred_element_type=jnp.float32,
    )
    width = residual.shape[1]
    offset = lax.axis_index("tp") * width
    own_part = lax.dynamic_slice_in_dim(partial_sum, offset, width, 1) + residual.astype(
        jnp.float32
    )
    placed = lax.dynamic_update_slice_in_dim(partial_sum, own_part, offset, 1)
    whole = lax.psum(placed.astype(jnp.bfloat16), "tp").astype(jnp.float32)
    hidden = lax.dynamic_slice_in_dim(whole, offset, width, 1)
    squares = jnp.sum(whole * whole, axis=1)
    inverse = lax.rsqrt(squares / D + 1e-06)
    level = jnp.sum(jnp.where(member, noise_level[0][None, :], 0), axis=1)
    onehot = (level[:, None] == jnp.arange(level_shift.shape[0], dtype=jnp.int32)[None, :]).astype(
        jnp.float32
    )
    shift = jnp.dot(onehot, level_shift, precision=lax.Precision.HIGHEST)
    normed = hidden * inverse[:, None] * norm_gain[None, :] * (1.0 + shift)
    return normed.astype(jnp.bfloat16)


def solution(mesh):
    placed = (
        P(("section", "srv"), "tp"),
        P(("section", "srv"), "tp"),
        P(("section", "srv"), "tp"),
        P(("section", "srv"), "tp"),
        P("tp", ("section", "srv")),
        P("tp"),
        P(None, "tp"),
        P("section", None),
        P("section", None),
    )
    return jax.shard_map(
        on_device,
        mesh=mesh,
        in_specs=placed,
        out_specs=P(("section", "srv"), "tp"),
        check_vma=False,
    )
```

profile of v0, /device:TPU:0, one launch (start us, length us, event | category | flops | bytes accessed | tf_op | source)
XLA Modules:
  0.0 211.0 jit_solution(15229370713892735644)
XLA Ops:
  8.2 1.1 copy.50
  11.4 3.9 %conditional.2 = (f32[2,1024]{1,0:T(2,128)}, f32[2,1024]{1,0:T(2,128)S(1)}, f32[2,1024,128]{2,1,0:T(8,128)S(1)}) conditional(s32[]{:T(128)} %convert_element_type.41, () %tuple.34, (pred[1024,128]{0,1:T(8,128)(4,1)S(1)}, bf16[128,256]{1,0:T(8,128)(2,1)S(1)}, bf16[2,1024,128]{2,1,0:T(8,128)(2,1)S(1)}, bf16[128,256]{1,0:T(8,128)(2,1)S(1)}) %tuple.84), branch_computations={%region_3.4_spmd, %region_4.7_spmd} | conditional | flops 136847360 | bytes 5333016 | solution.py:67
  12.4 1.3 convolution_add_fusion
  13.7 0.9 fusion.6
  15.3 74.7 %while.20 = (s32[]{:T(128)}, f32[2,1024]{1,0:T(2,128)}, f32[2,1024]{1,0:T(2,128)S(1)}, f32[2,1024,128]{2,1,0:T(8,128)S(1)}, bf16[2,128,256]{1,2,0:T(8,128)(2,1)S...) while((s32[]{:T(128)}, f32[2,1024]{1,0:T(2,128)}, ...), condition=%wide.region_13.14_spmd.clone, body=%wide.region_7.13_spmd.clone.sunk | while | flops 137629824 | bytes 7620895 | solution.py:105
  15.4 2.4 %collective-permute-start = (bf16[2,128,256]{1,2,0:T(8,128)(2,1)S(1)}, bf16[2,128,256]{1,2,0:T(8,128)(2,1)S(1)}, u32[]{:S(2)}, u32[]{:S(2)}) collective-permute-start(bf16[2,128,256]{1,2,0:T(8,128)(2,1)S(1)} %get-tuple-element.376), channel_id=1, source_target_pairs={{0,2},{2,4},{4,6},{6,8},{8,10},{10,12},{12,14},{14,16},{16,18},{18... | collective-permute-start | bytes 393224 | tf_op jit(solution)/shard_map/while/body/eval_jaxpr/ppermute | solution.py:14
  17.8 0.9 compare_and_fusion.4
  19.4 10.3 %collective-permute-start = (bf16[2,128,256]{1,2,0:T(8,128)(2,1)S(1)}, bf16[2,128,256]{1,2,0:T(8,128)(2,1)S(1)}, u32[]{:S(2)}, u32[]{:S(2)}) collective-permute-start(bf16[2,128,256]{1,2,0:T(8,128)(2,1)S(1)} %get-tuple-element.376), channel_id=1, source_target_pairs={{0,2},{2,4},{4,6},{6,8},{8,10},{10,12},{12,14},{14,16},{16,18},{18... | collective-permute-start | bytes 393224 | tf_op jit(solution)/shard_map/while/body/eval_jaxpr/ppermute | solution.py:14
  29.7 0.9 compare_and_fusion.4
  31.2 5.6 %collective-permute-start = (bf16[2,128,256]{1,2,0:T(8,128)(2,1)S(1)}, bf16[2,128,256]{1,2,0:T(8,128)(2,1)S(1)}, u32[]{:S(2)}, u32[]{:S(2)}) collective-permute-start(bf16[2,128,256]{1,2,0:T(8,128)(2,1)S(1)} %get-tuple-element.376), channel_id=1, source_target_pairs={{0,2},{2,4},{4,6},{6,8},{8,10},{10,12},{12,14},{14,16},{16,18},{18... | collective-permute-start | bytes 393224 | tf_op jit(solution)/shard_map/while/body/eval_jaxpr/ppermute | solution.py:14
  36.9 0.9 compare_and_fusion.4
  38.4 8.3 %collective-permute-start = (bf16[2,128,256]{1,2,0:T(8,128)(2,1)S(1)}, bf16[2,128,256]{1,2,0:T(8,128)(2,1)S(1)}, u32[]{:S(2)}, u32[]{:S(2)}) collective-permute-start(bf16[2,128,256]{1,2,0:T(8,128)(2,1)S(1)} %get-tuple-element.376), channel_id=1, source_target_pairs={{0,2},{2,4},{4,6},{6,8},{8,10},{10,12},{12,14},{14,16},{16,18},{18... | collective-permute-start | bytes 393224 | tf_op jit(solution)/shard_map/while/body/eval_jaxpr/ppermute | solution.py:14
  46.7 0.9 compare_and_fusion.4
  48.3 4.7 %collective-permute-start = (bf16[2,128,256]{1,2,0:T(8,128)(2,1)S(1)}, bf16[2,128,256]{1,2,0:T(8,128)(2,1)S(1)}, u32[]{:S(2)}, u32[]{:S(2)}) collective-permute-start(bf16[2,128,256]{1,2,0:T(8,128)(2,1)S(1)} %get-tuple-element.376), channel_id=1, source_target_pairs={{0,2},{2,4},{4,6},{6,8},{8,10},{10,12},{12,14},{14,16},{16,18},{18... | collective-permute-start | bytes 393224 | tf_op jit(solution)/shard_map/while/body/eval_jaxpr/ppermute | solution.py:14
  54.6 8.4 %collective-permute-start = (bf16[2,128,256]{1,2,0:T(8,128)(2,1)S(1)}, bf16[2,128,256]{1,2,0:T(8,128)(2,1)S(1)}, u32[]{:S(2)}, u32[]{:S(2)}) collective-permute-start(bf16[2,128,256]{1,2,0:T(8,128)(2,1)S(1)} %get-tuple-element.376), channel_id=1, source_target_pairs={{0,2},{2,4},{4,6},{6,8},{8,10},{10,12},{12,14},{14,16},{16,18},{18... | collective-permute-start | bytes 393224 | tf_op jit(solution)/shard_map/while/body/eval_jaxpr/ppermute | solution.py:14
  64.6 10.1 %collective-permute-start = (bf16[2,128,256]{1,2,0:T(8,128)(2,1)S(1)}, bf16[2,128,256]{1,2,0:T(8,128)(2,1)S(1)}, u32[]{:S(2)}, u32[]{:S(2)}) collective-permute-start(bf16[2,128,256]{1,2,0:T(8,128)(2,1)S(1)} %get-tuple-element.376), channel_id=1, source_target_pairs={{0,2},{2,4},{4,6},{6,8},{8,10},{10,12},{12,14},{14,16},{16,18},{18... | collective-permute-start | bytes 393224 | tf_op jit(solution)/shard_map/while/body/eval_jaxpr/ppermute | solution.py:14
  76.3 12.2 %collective-permute-start = (bf16[2,128,256]{1,2,0:T(8,128)(2,1)S(1)}, bf16[2,128,256]{1,2,0:T(8,128)(2,1)S(1)}, u32[]{:S(2)}, u32[]{:S(2)}) collective-permute-start(bf16[2,128,256]{1,2,0:T(8,128)(2,1)S(1)} %get-tuple-element.376), channel_id=1, source_target_pairs={{0,2},{2,4},{4,6},{6,8},{8,10},{10,12},{12,14},{14,16},{16,18},{18... | collective-permute-start | bytes 393224 | tf_op jit(solution)/shard_map/while/body/eval_jaxpr/ppermute | solution.py:14
  90.7 58.3 %all-gather.2.cloned.1.call-done = bf16[2048,4096]{1,0:T(8,128)(2,1)} async-done(((bf16[2048,256]{1,0:T(8,128)(2,1)}), bf16[2048,4096]{1,0:T(8,128)(2,1)}) %all-gather.2.cloned.1.call-update) | async-done | bytes 16777232 | tf_op jit(solution)/shard_map/all_gather | solution.py:109
  149.1 8.2 %fusion.34 = f32[128,4096]{1,0:T(8,128)S(1)} fusion(bf16[128,2048]{0,1:T(8,128)(2,1)S(1)} %bitcast.61, bf16[2048,4096]{1,0:T(8,128)(2,1)} %all-gather.2.cloned.1.call-done), kind=kOutput, calls=%fused_computation.65 | convolution fusion | flops 2147483648 | bytes 19398656 | tf_op jit(solution)/shard_map/dot_general | solution.py:107
  157.4 1.2 convert_element_type.47
  158.6 41.1 %all-reduce.2.cloned.1.call-done = bf16[128,4096]{1,0:T(8,128)(2,1)} async-done(((bf16[128,4096]{1,0:T(8,128)(2,1)}), bf16[128,4096]{1,0:T(8,128)(2,1)}) %all-reduce.2.cloned.1.call-update) | async-done | bytes 1048592 | tf_op jit(solution)/shard_map/psum | solution.py:118
  199.7 1.5 multiply_reduce_fusion
  201.3 1.4 convert_element_type.48
  202.7 1.4 fusion.27
  (81 shorter events, 9.2 us)
Async XLA Ops:
  6.5 196.2 %copy-start = (f32[8,2048]{1,0:T(8,128)S(1)}, f32[8,2048]{1,0:T(8,128)}, u32[]{:S(2)}) copy-start(f32[8,2048]{1,0:T(8,128)} %param.21) | copy-start | bytes 196612
  6.5 3.0 %copy-start.6 = (s32[1,4]{1,0:T(1,128)S(1)}, s32[1,4]{1,0:T(1,128)}, u32[]{:S(2)}) copy-start(s32[1,4]{1,0:T(1,128)} %param.22) | copy-start | bytes 52
  6.5 3.0 %copy-start.5 = (s32[1,4]{1,0:T(1,128)S(1)}, s32[1,4]{1,0:T(1,128)}, u32[]{:S(2)}) copy-start(s32[1,4]{1,0:T(1,128)} %param.23) | copy-start | bytes 52
  6.5 4.6 %copy-start.2 = (bf16[128,256]{1,0:T(8,128)(2,1)S(1)}, bf16[128,256]{1,0:T(8,128)(2,1)}, u32[]{:S(2)}) copy-start(bf16[128,256]{1,0:T(8,128)(2,1)} %param.16) | copy-start | bytes 196612
  6.5 4.7 %copy-start.3 = (bf16[128,256]{1,0:T(8,128)(2,1)S(1)}, bf16[128,256]{1,0:T(8,128)(2,1)}, u32[]{:S(2)}) copy-start(bf16[128,256]{1,0:T(8,128)(2,1)} %param.17) | copy-start | bytes 196612
  6.5 142.5 %all-gather.2.cloned.1.call-start = ((), (), s32[]{:S(2)}) async-start(), calls=%async_computation | async-start | bytes 17825792 | tf_op jit(solution)/shard_map/all_gather | solution.py:109
  7.3 192.4 %all-reduce.2.cloned.1.call-start = ((), (), s32[]{:S(2)}) async-start(), calls=%async_computation.1 | async-start | bytes 2097152 | tf_op jit(solution)/shard_map/psum | solution.py:118
  15.4 3.9 %collective-permute-start = (bf16[2,128,256]{1,2,0:T(8,128)(2,1)S(1)}, bf16[2,128,256]{1,2,0:T(8,128)(2,1)S(1)}, u32[]{:S(2)}, u32[]{:S(2)}) collective-permute-start(bf16[2,128,256]{1,2,0:T(8,128)(2,1)S(1)} %get-tuple-element.376), channel_id=1, source_target_pairs={{0,2},{2,4},{4,6},{6,8},{8,10},{10,12},{12,14},{14,16},{16,18},{18... | collective-permute-start | bytes 393224 | tf_op jit(solution)/shard_map/while/body/eval_jaxpr/ppermute | solution.py:14
  19.4 11.8 %collective-permute-start = (bf16[2,128,256]{1,2,0:T(8,128)(2,1)S(1)}, bf16[2,128,256]{1,2,0:T(8,128)(2,1)S(1)}, u32[]{:S(2)}, u32[]{:S(2)}) collective-permute-start(bf16[2,128,256]{1,2,0:T(8,128)(2,1)S(1)} %get-tuple-element.376), channel_id=1, source_target_pairs={{0,2},{2,4},{4,6},{6,8},{8,10},{10,12},{12,14},{14,16},{16,18},{18... | collective-permute-start | bytes 393224 | tf_op jit(solution)/shard_map/while/body/eval_jaxpr/ppermute | solution.py:14
  31.2 7.1 %collective-permute-start = (bf16[2,128,256]{1,2,0:T(8,128)(2,1)S(1)}, bf16[2,128,256]{1,2,0:T(8,128)(2,1)S(1)}, u32[]{:S(2)}, u32[]{:S(2)}) collective-permute-start(bf16[2,128,256]{1,2,0:T(8,128)(2,1)S(1)} %get-tuple-element.376), channel_id=1, source_target_pairs={{0,2},{2,4},{4,6},{6,8},{8,10},{10,12},{12,14},{14,16},{16,18},{18... | collective-permute-start | bytes 393224 | tf_op jit(solution)/shard_map/while/body/eval_jaxpr/ppermute | solution.py:14
  38.4 9.8 %collective-permute-start = (bf16[2,128,256]{1,2,0:T(8,128)(2,1)S(1)}, bf16[2,128,256]{1,2,0:T(8,128)(2,1)S(1)}, u32[]{:S(2)}, u32[]{:S(2)}) collective-permute-start(bf16[2,128,256]{1,2,0:T(8,128)(2,1)S(1)} %get-tuple-element.376), channel_id=1, source_target_pairs={{0,2},{2,4},{4,6},{6,8},{8,10},{10,12},{12,14},{14,16},{16,18},{18... | collective-permute-start | bytes 393224 | tf_op jit(solution)/shard_map/while/body/eval_jaxpr/ppermute | solution.py:14
  48.3 6.3 %collective-permute-start = (bf16[2,128,256]{1,2,0:T(8,128)(2,1)S(1)}, bf16[2,128,256]{1,2,0:T(8,128)(2,1)S(1)}, u32[]{:S(2)}, u32[]{:S(2)}) collective-permute-start(bf16[2,128,256]{1,2,0:T(8,128)(2,1)S(1)} %get-tuple-element.376), channel_id=1, source_target_pairs={{0,2},{2,4},{4,6},{6,8},{8,10},{10,12},{12,14},{14,16},{16,18},{18... | collective-permute-start | bytes 393224 | tf_op jit(solution)/shard_map/while/body/eval_jaxpr/ppermute | solution.py:14
  54.6 10.0 %collective-permute-start = (bf16[2,128,256]{1,2,0:T(8,128)(2,1)S(1)}, bf16[2,128,256]{1,2,0:T(8,128)(2,1)S(1)}, u32[]{:S(2)}, u32[]{:S(2)}) collective-permute-start(bf16[2,128,256]{1,2,0:T(8,128)(2,1)S(1)} %get-tuple-element.376), channel_id=1, source_target_pairs={{0,2},{2,4},{4,6},{6,8},{8,10},{10,12},{12,14},{14,16},{16,18},{18... | collective-permute-start | bytes 393224 | tf_op jit(solution)/shard_map/while/body/eval_jaxpr/ppermute | solution.py:14
  64.6 11.6 %collective-permute-start = (bf16[2,128,256]{1,2,0:T(8,128)(2,1)S(1)}, bf16[2,128,256]{1,2,0:T(8,128)(2,1)S(1)}, u32[]{:S(2)}, u32[]{:S(2)}) collective-permute-start(bf16[2,128,256]{1,2,0:T(8,128)(2,1)S(1)} %get-tuple-element.376), channel_id=1, source_target_pairs={{0,2},{2,4},{4,6},{6,8},{8,10},{10,12},{12,14},{14,16},{16,18},{18... | collective-permute-start | bytes 393224 | tf_op jit(solution)/shard_map/while/body/eval_jaxpr/ppermute | solution.py:14
  76.3 13.7 %collective-permute-start = (bf16[2,128,256]{1,2,0:T(8,128)(2,1)S(1)}, bf16[2,128,256]{1,2,0:T(8,128)(2,1)S(1)}, u32[]{:S(2)}, u32[]{:S(2)}) collective-permute-start(bf16[2,128,256]{1,2,0:T(8,128)(2,1)S(1)} %get-tuple-element.376), channel_id=1, source_target_pairs={{0,2},{2,4},{4,6},{6,8},{8,10},{10,12},{12,14},{14,16},{16,18},{18... | collective-permute-start | bytes 393224 | tf_op jit(solution)/shard_map/while/body/eval_jaxpr/ppermute | solution.py:14
  149.0 8.2 %copy-start.1 = (bf16[128,2048]{1,0:T(8,128)(2,1)S(1)}, bf16[128,2048]{1,0:T(8,128)(2,1)}, u32[]{:S(2)}) copy-start(bf16[128,2048]{1,0:T(8,128)(2,1)} %param.18) | copy-start | bytes 1572868
  158.6 44.1 %copy-start.4 = (f32[2048]{0:T(1024)S(1)}, f32[2048]{0:T(1024)}, u32[]{:S(2)}) copy-start(f32[2048]{0:T(1024)} %param.20) | copy-start | bytes 24580
Sparse Core Ops, SparseCore 0:
  9.5 139.4 all-gather.1
  158.7 40.9 all-reduce.1
where the time goes:
time: 212 us; the launch traced here: 211 us
  waiting for transfers between devices  100 us (47%)
  starting transfers between devices  62.1 us (29%)
  other arithmetic  15.7 us (7%)
  between operations  14.2 us (7%)
  matrix products  11.3 us (5%)
  loops' own time  5.64 us (3%)
    ppermute x8, starting transfers between devices, shifted(): return lax.ppermute(block, axis, route)  62 us
    all_gather x1, waiting for transfers between devices, on_device(): lax.all_gather(out_weight, ('section', 'srv'), axis=1, tiled=True)  58.3 us
    psum x1, waiting for transfers between devices, on_device(): whole = lax.psum(placed.astype(jnp.bfloat16), 'tp').astype(jnp.float32)  41.1 us
    dot_general x1, matrix products, on_device(): jnp.dot(attended, lax.all_gather(out_weight, ('section', 'srv'), axis=1,...  8.18 us
    and x9, other arithmetic, absorb(): (key_pos[None, :] >= row_first[:, None]) & (key_pos[None, :] < row_limit[...  7.8 us
    another operation x1, loops' own time, on_device(): lax.fori_loop(1, span, turn_step, (carry, jnp.stack([keys, values], axis=...  5.48 us
  transfers between devices with their start and end apart: 10, of which 2 were waited for; matrix products, arithmetic and copies ran while one was open for 7% of the time, Pallas kernels for 0%

commit v1 on v0

--- a/solution.py
+++ b/solution.py
@@ -115,7 +115,7 @@
         jnp.float32
     )
     placed = lax.dynamic_update_slice_in_dim(partial_sum, own_part, offset, 1)
-    whole = lax.psum(placed.astype(jnp.bfloat16), "tp").astype(jnp.float32)
+    whole = jnp.sum(lax.all_gather(placed.astype(jnp.bfloat16), "tp"), axis=0).astype(jnp.float32)
     hidden = lax.dynamic_slice_in_dim(whole, offset, width, 1)
     squares = jnp.sum(whole * whole, axis=1)
     inverse = lax.rsqrt(squares / D + 1e-06)

time: 212 us -> 206 us (0.972)
  waiting for transfers between devices: 100 us -> 93.7 us
    psum x1 -> x0, waiting for transfers between devices: 41.1 us -> none  [on_device(): whole = lax.psum(placed.astype(jnp.bfloat16), 'tp').astype(jnp.float32)]
    all_gather x0 -> x1, waiting for transfers between devices: none -> 34 us  [on_device(): lax.all_gather(placed.astype(jnp.bfloat16), 'tp')]
where the time goes in v1:
time: 206 us; the launch traced here: 204 us
  waiting for transfers between devices  93.7 us (45%)
  starting transfers between devices  62.1 us (30%)
  other arithmetic  15.3 us (7%)
  between operations  14.2 us (7%)
  matrix products  11.3 us (5%)
  loops' own time  5.64 us (3%)
  local copies, waits for them, and re-layouts  2.1 us (1%)
    ppermute x8, starting transfers between devices, shifted(): return lax.ppermute(block, axis, route)  62 us
    all_gather x1, waiting for transfers between devices, on_device(): lax.all_gather(out_weight, ('section', 'srv'), axis=1, tiled=True)  59 us
    all_gather x1, waiting for transfers between devices, on_device(): lax.all_gather(placed.astype(jnp.bfloat16), 'tp')  34 us
    dot_general x1, matrix products, on_device(): jnp.dot(attended, lax.all_gather(out_weight, ('section', 'srv'), axis=1,...  8.18 us
    and x9, other arithmetic, absorb(): (key_pos[None, :] >= row_first[:, None]) & (key_pos[None, :] < row_limit[...  7.8 us
    another operation x1, loops' own time, on_device(): lax.fori_loop(1, span, turn_step, (carry, jnp.stack([keys, values], axis=...  5.48 us
  transfers between devices with their start and end apart: 10, of which 2 were waited for; matrix products, arithmetic and copies ran while one was open for 7% of the time, Pallas kernels for 0%

profile of v1, /device:TPU:0, one launch (start us, length us, event | category | flops | bytes accessed | tf_op | source)
XLA Modules:
  0.0 204.2 jit_solution(7835478841868971317)
XLA Ops:
  8.2 1.1 copy.50
  11.4 3.9 %conditional.2 = (f32[2,1024]{1,0:T(2,128)}, f32[2,1024]{1,0:T(2,128)S(1)}, f32[2,1024,128]{2,1,0:T(8,128)S(1)}) conditional(s32[]{:T(128)} %convert_element_type.43, () %tuple.34, (pred[1024,128]{0,1:T(8,128)(4,1)S(1)}, bf16[128,256]{1,0:T(8,128)(2,1)S(1)}, bf16[2,1024,128]{2,1,0:T(8,128)(2,1)S(1)}, bf16[128,256]{1,0:T(8,128)(2,1)S(1)}) %tuple.84), branch_computations={%region_3.4_spmd, %region_4.7_spmd} | conditional | flops 136847360 | bytes 5333016 | solution.py:67
  12.4 1.3 convolution_add_fusion
  13.7 0.9 fusion.6
  15.3 74.7 %while.20 = (s32[]{:T(128)}, f32[2,1024]{1,0:T(2,128)}, f32[2,1024]{1,0:T(2,128)S(1)}, f32[2,1024,128]{2,1,0:T(8,128)S(1)}, bf16[2,128,256]{1,2,0:T(8,128)(2,1)S...) while((s32[]{:T(128)}, f32[2,1024]{1,0:T(2,128)}, ...), condition=%wide.region_13.14_spmd.clone, body=%wide.region_7.13_spmd.clone.sunk | while | flops 137629824 | bytes 7620895 | solution.py:105
  15.4 2.4 %collective-permute-start = (bf16[2,128,256]{1,2,0:T(8,128)(2,1)S(1)}, bf16[2,128,256]{1,2,0:T(8,128)(2,1)S(1)}, u32[]{:S(2)}, u32[]{:S(2)}) collective-permute-start(bf16[2,128,256]{1,2,0:T(8,128)(2,1)S(1)} %get-tuple-element.376), channel_id=1, source_target_pairs={{0,2},{2,4},{4,6},{6,8},{8,10},{10,12},{12,14},{14,16},{16,18},{18... | collective-permute-start | bytes 393224 | tf_op jit(solution)/shard_map/while/body/eval_jaxpr/ppermute | solution.py:14
  17.8 0.9 compare_and_fusion.4
  19.4 10.3 %collective-permute-start = (bf16[2,128,256]{1,2,0:T(8,128)(2,1)S(1)}, bf16[2,128,256]{1,2,0:T(8,128)(2,1)S(1)}, u32[]{:S(2)}, u32[]{:S(2)}) collective-permute-start(bf16[2,128,256]{1,2,0:T(8,128)(2,1)S(1)} %get-tuple-element.376), channel_id=1, source_target_pairs={{0,2},{2,4},{4,6},{6,8},{8,10},{10,12},{12,14},{14,16},{16,18},{18... | collective-permute-start | bytes 393224 | tf_op jit(solution)/shard_map/while/body/eval_jaxpr/ppermute | solution.py:14
  29.6 0.9 compare_and_fusion.4
  31.2 5.6 %collective-permute-start = (bf16[2,128,256]{1,2,0:T(8,128)(2,1)S(1)}, bf16[2,128,256]{1,2,0:T(8,128)(2,1)S(1)}, u32[]{:S(2)}, u32[]{:S(2)}) collective-permute-start(bf16[2,128,256]{1,2,0:T(8,128)(2,1)S(1)} %get-tuple-element.376), channel_id=1, source_target_pairs={{0,2},{2,4},{4,6},{6,8},{8,10},{10,12},{12,14},{14,16},{16,18},{18... | collective-permute-start | bytes 393224 | tf_op jit(solution)/shard_map/while/body/eval_jaxpr/ppermute | solution.py:14
  36.9 0.9 compare_and_fusion.4
  38.4 8.3 %collective-permute-start = (bf16[2,128,256]{1,2,0:T(8,128)(2,1)S(1)}, bf16[2,128,256]{1,2,0:T(8,128)(2,1)S(1)}, u32[]{:S(2)}, u32[]{:S(2)}) collective-permute-start(bf16[2,128,256]{1,2,0:T(8,128)(2,1)S(1)} %get-tuple-element.376), channel_id=1, source_target_pairs={{0,2},{2,4},{4,6},{6,8},{8,10},{10,12},{12,14},{14,16},{16,18},{18... | collective-permute-start | bytes 393224 | tf_op jit(solution)/shard_map/while/body/eval_jaxpr/ppermute | solution.py:14
  46.7 0.9 compare_and_fusion.4
  48.3 4.7 %collective-permute-start = (bf16[2,128,256]{1,2,0:T(8,128)(2,1)S(1)}, bf16[2,128,256]{1,2,0:T(8,128)(2,1)S(1)}, u32[]{:S(2)}, u32[]{:S(2)}) collective-permute-start(bf16[2,128,256]{1,2,0:T(8,128)(2,1)S(1)} %get-tuple-element.376), channel_id=1, source_target_pairs={{0,2},{2,4},{4,6},{6,8},{8,10},{10,12},{12,14},{14,16},{16,18},{18... | collective-permute-start | bytes 393224 | tf_op jit(solution)/shard_map/while/body/eval_jaxpr/ppermute | solution.py:14
  53.0 0.9 compare_and_fusion.4
  54.6 8.4 %collective-permute-start = (bf16[2,128,256]{1,2,0:T(8,128)(2,1)S(1)}, bf16[2,128,256]{1,2,0:T(8,128)(2,1)S(1)}, u32[]{:S(2)}, u32[]{:S(2)}) collective-permute-start(bf16[2,128,256]{1,2,0:T(8,128)(2,1)S(1)} %get-tuple-element.376), channel_id=1, source_target_pairs={{0,2},{2,4},{4,6},{6,8},{8,10},{10,12},{12,14},{14,16},{16,18},{18... | collective-permute-start | bytes 393224 | tf_op jit(solution)/shard_map/while/body/eval_jaxpr/ppermute | solution.py:14
  64.6 10.0 %collective-permute-start = (bf16[2,128,256]{1,2,0:T(8,128)(2,1)S(1)}, bf16[2,128,256]{1,2,0:T(8,128)(2,1)S(1)}, u32[]{:S(2)}, u32[]{:S(2)}) collective-permute-start(bf16[2,128,256]{1,2,0:T(8,128)(2,1)S(1)} %get-tuple-element.376), channel_id=1, source_target_pairs={{0,2},{2,4},{4,6},{6,8},{8,10},{10,12},{12,14},{14,16},{16,18},{18... | collective-permute-start | bytes 393224 | tf_op jit(solution)/shard_map/while/body/eval_jaxpr/ppermute | solution.py:14
  76.2 12.2 %collective-permute-start = (bf16[2,128,256]{1,2,0:T(8,128)(2,1)S(1)}, bf16[2,128,256]{1,2,0:T(8,128)(2,1)S(1)}, u32[]{:S(2)}, u32[]{:S(2)}) collective-permute-start(bf16[2,128,256]{1,2,0:T(8,128)(2,1)S(1)} %get-tuple-element.376), channel_id=1, source_target_pairs={{0,2},{2,4},{4,6},{6,8},{8,10},{10,12},{12,14},{14,16},{16,18},{18... | collective-permute-start | bytes 393224 | tf_op jit(solution)/shard_map/while/body/eval_jaxpr/ppermute | solution.py:14
  90.7 59.0 %all-gather.4.cloned.1.call-done = bf16[2048,4096]{1,0:T(8,128)(2,1)} async-done(((bf16[2048,256]{1,0:T(8,128)(2,1)}), bf16[2048,4096]{1,0:T(8,128)(2,1)}) %all-gather.4.cloned.1.call-update) | async-done | bytes 16777232 | tf_op jit(solution)/shard_map/all_gather | solution.py:109
  149.7 8.2 %fusion.34 = f32[128,4096]{1,0:T(8,128)S(1)} fusion(bf16[128,2048]{0,1:T(8,128)(2,1)S(1)} %bitcast.62, bf16[2048,4096]{1,0:T(8,128)(2,1)} %all-gather.4.cloned.1.call-done), kind=kOutput, calls=%fused_computation.65 | convolution fusion | flops 2147483648 | bytes 19398656 | tf_op jit(solution)/shard_map/dot_general | solution.py:107
  158.0 1.1 convert_element_type.49
  159.2 34.0 %all-gather.6.cloned.1.call-done = bf16[256,4096]{1,0:T(8,128)(2,1)} async-done(((bf16[128,4096]{1,0:T(8,128)(2,1)}), bf16[256,4096]{1,0:T(8,128)(2,1)}) %all-gather.6.cloned.1.call-update) | async-done | bytes 2097168 | tf_op jit(solution)/shard_map/all_gather | solution.py:118
  193.2 2.1 %reduce_sum.58 = bf16[128,4096]{1,0:T(8,128)(2,1)S(1)} reduce(bf16[2,128,4096]{2,1,0:T(8,128)(2,1)} %bitcast.64, bf16[]{:T(256)} %constant.93.clone.1), dimensions={0}, to_apply=%region_14.15 | reduce | flops 524288 | bytes 3145730 | tf_op jit(solution)/shard_map/reduce_sum | solution.py:118
  196.0 1.4 fusion.27
  (82 shorter events, 9.0 us)
Async XLA Ops:
  6.5 189.3 %copy-start = (f32[8,2048]{1,0:T(8,128)S(1)}, f32[8,2048]{1,0:T(8,128)}, u32[]{:S(2)}) copy-start(f32[8,2048]{1,0:T(8,128)} %param.21) | copy-start | bytes 196612
  6.5 3.0 %copy-start.6 = (s32[1,4]{1,0:T(1,128)S(1)}, s32[1,4]{1,0:T(1,128)}, u32[]{:S(2)}) copy-start(s32[1,4]{1,0:T(1,128)} %param.22) | copy-start | bytes 52
  6.5 3.0 %copy-start.5 = (s32[1,4]{1,0:T(1,128)S(1)}, s32[1,4]{1,0:T(1,128)}, u32[]{:S(2)}) copy-start(s32[1,4]{1,0:T(1,128)} %param.23) | copy-start | bytes 52
  6.5 4.6 %copy-start.2 = (bf16[128,256]{1,0:T(8,128)(2,1)S(1)}, bf16[128,256]{1,0:T(8,128)(2,1)}, u32[]{:S(2)}) copy-start(bf16[128,256]{1,0:T(8,128)(2,1)} %param.16) | copy-start | bytes 196612
  6.5 4.7 %copy-start.3 = (bf16[128,256]{1,0:T(8,128)(2,1)S(1)}, bf16[128,256]{1,0:T(8,128)(2,1)}, u32[]{:S(2)}) copy-start(bf16[128,256]{1,0:T(8,128)(2,1)} %param.17) | copy-start | bytes 196612
  6.5 143.1 %all-gather.4.cloned.1.call-start = ((), (), s32[]{:S(2)}) async-start(), calls=%async_computation | async-start | bytes 17825792 | tf_op jit(solution)/shard_map/all_gather | solution.py:109
  7.3 185.9 %all-gather.6.cloned.1.call-start = ((), (), s32[]{:S(2)}) async-start(), calls=%async_computation.1 | async-start | bytes 3145728 | tf_op jit(solution)/shard_map/all_gather | solution.py:118
  15.4 3.9 %collective-permute-start = (bf16[2,128,256]{1,2,0:T(8,128)(2,1)S(1)}, bf16[2,128,256]{1,2,0:T(8,128)(2,1)S(1)}, u32[]{:S(2)}, u32[]{:S(2)}) collective-permute-start(bf16[2,128,256]{1,2,0:T(8,128)(2,1)S(1)} %get-tuple-element.376), channel_id=1, source_target_pairs={{0,2},{2,4},{4,6},{6,8},{8,10},{10,12},{12,14},{14,16},{16,18},{18... | collective-permute-start | bytes 393224 | tf_op jit(solution)/shard_map/while/body/eval_jaxpr/ppermute | solution.py:14
  19.4 11.8 %collective-permute-start = (bf16[2,128,256]{1,2,0:T(8,128)(2,1)S(1)}, bf16[2,128,256]{1,2,0:T(8,128)(2,1)S(1)}, u32[]{:S(2)}, u32[]{:S(2)}) collective-permute-start(bf16[2,128,256]{1,2,0:T(8,128)(2,1)S(1)} %get-tuple-element.376), channel_id=1, source_target_pairs={{0,2},{2,4},{4,6},{6,8},{8,10},{10,12},{12,14},{14,16},{16,18},{18... | collective-permute-start | bytes 393224 | tf_op jit(solution)/shard_map/while/body/eval_jaxpr/ppermute | solution.py:14
  31.2 7.1 %collective-permute-start = (bf16[2,128,256]{1,2,0:T(8,128)(2,1)S(1)}, bf16[2,128,256]{1,2,0:T(8,128)(2,1)S(1)}, u32[]{:S(2)}, u32[]{:S(2)}) collective-permute-start(bf16[2,128,256]{1,2,0:T(8,128)(2,1)S(1)} %get-tuple-element.376), channel_id=1, source_target_pairs={{0,2},{2,4},{4,6},{6,8},{8,10},{10,12},{12,14},{14,16},{16,18},{18... | collective-permute-start | bytes 393224 | tf_op jit(solution)/shard_map/while/body/eval_jaxpr/ppermute | solution.py:14
  38.4 9.8 %collective-permute-start = (bf16[2,128,256]{1,2,0:T(8,128)(2,1)S(1)}, bf16[2,128,256]{1,2,0:T(8,128)(2,1)S(1)}, u32[]{:S(2)}, u32[]{:S(2)}) collective-permute-start(bf16[2,128,256]{1,2,0:T(8,128)(2,1)S(1)} %get-tuple-element.376), channel_id=1, source_target_pairs={{0,2},{2,4},{4,6},{6,8},{8,10},{10,12},{12,14},{14,16},{16,18},{18... | collective-permute-start | bytes 393224 | tf_op jit(solution)/shard_map/while/body/eval_jaxpr/ppermute | solution.py:14
  48.3 6.3 %collective-permute-start = (bf16[2,128,256]{1,2,0:T(8,128)(2,1)S(1)}, bf16[2,128,256]{1,2,0:T(8,128)(2,1)S(1)}, u32[]{:S(2)}, u32[]{:S(2)}) collective-permute-start(bf16[2,128,256]{1,2,0:T(8,128)(2,1)S(1)} %get-tuple-element.376), channel_id=1, source_target_pairs={{0,2},{2,4},{4,6},{6,8},{8,10},{10,12},{12,14},{14,16},{16,18},{18... | collective-permute-start | bytes 393224 | tf_op jit(solution)/shard_map/while/body/eval_jaxpr/ppermute | solution.py:14
  54.6 10.0 %collective-permute-start = (bf16[2,128,256]{1,2,0:T(8,128)(2,1)S(1)}, bf16[2,128,256]{1,2,0:T(8,128)(2,1)S(1)}, u32[]{:S(2)}, u32[]{:S(2)}) collective-permute-start(bf16[2,128,256]{1,2,0:T(8,128)(2,1)S(1)} %get-tuple-element.376), channel_id=1, source_target_pairs={{0,2},{2,4},{4,6},{6,8},{8,10},{10,12},{12,14},{14,16},{16,18},{18... | collective-permute-start | bytes 393224 | tf_op jit(solution)/shard_map/while/body/eval_jaxpr/ppermute | solution.py:14
  64.6 11.5 %collective-permute-start = (bf16[2,128,256]{1,2,0:T(8,128)(2,1)S(1)}, bf16[2,128,256]{1,2,0:T(8,128)(2,1)S(1)}, u32[]{:S(2)}, u32[]{:S(2)}) collective-permute-start(bf16[2,128,256]{1,2,0:T(8,128)(2,1)S(1)} %get-tuple-element.376), channel_id=1, source_target_pairs={{0,2},{2,4},{4,6},{6,8},{8,10},{10,12},{12,14},{14,16},{16,18},{18... | collective-permute-start | bytes 393224 | tf_op jit(solution)/shard_map/while/body/eval_jaxpr/ppermute | solution.py:14
  76.2 13.8 %collective-permute-start = (bf16[2,128,256]{1,2,0:T(8,128)(2,1)S(1)}, bf16[2,128,256]{1,2,0:T(8,128)(2,1)S(1)}, u32[]{:S(2)}, u32[]{:S(2)}) collective-permute-start(bf16[2,128,256]{1,2,0:T(8,128)(2,1)S(1)} %get-tuple-element.376), channel_id=1, source_target_pairs={{0,2},{2,4},{4,6},{6,8},{8,10},{10,12},{12,14},{14,16},{16,18},{18... | collective-permute-start | bytes 393224 | tf_op jit(solution)/shard_map/while/body/eval_jaxpr/ppermute | solution.py:14
  149.7 8.2 %copy-start.1 = (bf16[128,2048]{1,0:T(8,128)(2,1)S(1)}, bf16[128,2048]{1,0:T(8,128)(2,1)}, u32[]{:S(2)}) copy-start(bf16[128,2048]{1,0:T(8,128)(2,1)} %param.18) | copy-start | bytes 1572868
  195.3 0.7 copy-start.4
Sparse Core Ops, SparseCore 0:
  9.5 140.1 all-gather.3
  159.3 33.8 all-gather.5
